TPU v7x, 32 devices: a whole 2x2x4 slice. The times are simulated.
32 devices in a mesh: row: 2 (over core), col: 8 (over z, x), mp: 2 (over y).
Axes of the slice: x: 2, y: 2, z: 4, core: 2. Of those that a mesh axis runs over, the one named last changes fastest.
Arguments:
- video: bfloat16 [3, 4, 48, 3072], P(None, None, 'row', 'col'), may hold values from -6 to 6
- grad_tokens: bfloat16 [2, 4, 256, 1024], P(None, 'row', 'col', 'mp'), may hold values from -6 to 6
- weight: bfloat16 [3072, 1024], P(None, 'mp'), may hold values from -0.1875 to 0.1875
Outputs:
- video_grad: float32 [3, 4, 48, 3072], P(None, 'mp', 'row', 'col')
- weight_grad: float32 [3072, 1024], P(('row', 'col'), 'mp')
All inputs are finite; a program needn't handle non-finite values.
Results may differ from a plain program's by a relative error of at most 0.0003.
Values may be sent and summed in bfloat16 or wider, within the bound.
No kernel may reach another device: no remote copies, remote signals or barrier semaphores. Data moves between devices by JAX's collectives and lax.ppermute only.
A program may use at most 64 MiB of HBM per device.

v0:
```python
import functools

import jax
import jax.numpy as jnp
import numpy as np
from jax import lax
from jax.experimental import pallas as pl
from jax.experimental.pallas import tpu as pltpu
from jax.sharding import PartitionSpec as P

KT, KS, ST, SS = 4, 16, 2, 12
LAP = (KS - SS) // 2

VMEM = pltpu.VMEM


def grant(mib):
    return pltpu.CompilerParams(vmem_limit_bytes=mib << 20)


def swap(x, axis, bit):
    n = lax.axis_size(axis)
    return lax.ppermute(x, axis, [(i, i ^ bit) for i in range(n)])


def shift(x, axis, by):
    n = lax.axis_size(axis)
    return lax.ppermute(x, axis, [(i, i + by) for i in range(n) if 0 <= i + by < n])


def rotate(x, axis, by):
    n = lax.axis_size(axis)
    return lax.ppermute(x, axis, [(i, (i + by) % n) for i in range(n)])


def grid_of(rows, columns):
    return (
        lax.broadcasted_iota(jnp.int32, (rows, columns), 0),
        lax.broadcasted_iota(jnp.int32, (rows, columns), 1),
    )


def zero_one(mask):
    return jnp.where(mask, 1.0, 0.0).astype(jnp.bfloat16)


def fold_matrix(cols):
    n, x = grid_of(KS * cols, SS * cols)
    return zero_one(SS * lax.rem(n, cols) + lax.div(n, cols) - LAP == x)


def unfold_matrix(cols):
    width = SS * cols
    x, n = grid_of(width + 128, KS * cols)
    x = jnp.where(x < width + 64, x, x - width - 128)
    return zero_one(SS * lax.rem(n, cols) + lax.div(n, cols) - LAP == x)


def edge_rows(groups, cols, first):
    k, n = grid_of(16, groups * cols)
    firsts = (k >= groups) & (k < 2 * groups) & (n == (k - groups) * cols)
    lasts = (k < groups) & (n == k * cols + cols - 1)
    return zero_one(firsts & first | lasts & jnp.logical_not(first))


def lap_rows(images, height, lap, at):
    k, n = grid_of(lap, images * height)
    return zero_one((k < images * LAP) & (n == lax.div(k, LAP) * height + lax.rem(k, LAP) + at))


def row_tables(channels, frames, height, steps, rows, nr, nc, block, touched):
    inside, lap = channels * frames * height, halo_rows(channels, frames)
    m = np.zeros((nc, steps, rows, nr, touched, inside + 2 * lap), np.float32)
    for c, t, i, r, q in np.ndindex(*m.shape[:-1]):
        triple = (r * nc + c) * block // KS + q
        ch, a, b = triple // (KT * KS), triple // KS % KT, triple % KS
        f, y = ST * t + a - 1, SS * i + b - LAP
        if ch < channels and 0 <= f < frames:
            image = ch * frames + f
            if y < 0:
                k = inside + image * LAP + y + LAP
            elif y >= height:
                k = inside + lap + image * LAP + y - height
            else:
                k = image * height + y
            m[c, t, i, r, q, k] = 1
    m = m.reshape(nc, -1, m.shape[-1])
    used = m.any(-1)
    places = -(-used.sum(1).max() // 8) * 8
    table = np.zeros((nc, places, m.shape[-1]), np.float32)
    spread = np.zeros((nc, m.shape[1], places), np.float32)
    for c in range(nc):
        for place, row in enumerate(np.flatnonzero(used[c])):
            table[c, place] = m[c, row]
            spread[c, row, place] = 1
    return jnp.asarray(table, jnp.bfloat16), jnp.asarray(spread, jnp.bfloat16)


def halo_rows(channels, frames):
    return -(-channels * frames * LAP // 16) * 16


def exact(a, b):
    return jnp.dot(a, b, preferred_element_type=jnp.float32).astype(jnp.bfloat16)


def even_column():
    return lax.rem(lax.axis_index("col"), 2) == 0


def prep_kernel(dims, video_ref, flat_ref, table_ref, spread_ref, video_out, flat_out, table_out, spread_out, edge_ref, *refs):
    split, images, height, groups, cols = dims
    halos, sem = refs[:-1], refs[-1]
    spread = spread_ref.at[lax.axis_index("col")]
    pairs = ((flat_ref, flat_out), (video_ref, video_out), (table_ref, table_out), (spread, spread_out))
    moves = [pltpu.make_async_copy(a, b, sem.at[k]) for k, (a, b) in enumerate(pairs)]
    for move in moves:
        move.start()
    picked = edge_rows(groups, cols, even_column())
    lap = halos[0].shape[0]
    if split == 2:
        at = jnp.where(lax.axis_index("row") == 0, height - LAP, 0)
        rows = [lap_rows(images, height, lap, at)]
    else:
        rows = [lap_rows(images, height, lap, at) for at in (0, height - LAP)]
    moves[0].wait()
    edge_ref[...] = exact(picked, flat_out[...])
    moves[1].wait()
    for row, halo in zip(rows, halos):
        halo[...] = exact(row, video_out[...])
    moves[2].wait()
    moves[3].wait()


def slab_kernel(split, table_ref, video_ref, weight_ref, *refs):
    halos, out_ref, weight_out, v_ref, rows_ref, sem = refs[:-5], *refs[-5:]
    move = pltpu.make_async_copy(weight_ref.at[: weight_out.shape[0]], weight_out, sem.at[0])
    move.start()
    inside, lap = video_ref.shape[0], halos[0].shape[0]
    v_ref[:inside] = video_ref[...]
    if split == 2:
        row = lax.axis_index("row")
        halo = halos[0][...]
        zero = jnp.zeros_like(halo)
        v_ref[inside : inside + lap] = zero
        v_ref[inside + lap :] = zero

        @pl.when(row == 1)
        def _():
            v_ref[inside : inside + lap] = halo

        @pl.when(row == 0)
        def _():
            v_ref[inside + lap :] = halo
    else:
        v_ref[inside : inside + lap] = halos[0][...]
        v_ref[inside + lap :] = halos[1][...]
    moves = [move]
    for k in range(out_ref.shape[0]):
        rows_ref[k] = exact(table_ref[k], v_ref[...])
        moves.append(pltpu.make_async_copy(rows_ref.at[k], out_ref.at[k], sem.at[k + 1]))
        moves[-1].start()
    for move in moves:
        move.wait()


def video_kernel(dims, first_ref, w_ref, g_ref, beside_ref, edge_ref, *refs):
    steps, rows, cols, parts, split = dims
    keep_ref, send_ref = refs[:2]
    halos = refs[2:-5]
    p_ref, f_ref, t_ref, load_ref, sem = refs[-5:]
    count = steps * rows * cols
    channels, patch = p_ref.shape[0], p_ref.shape[2]
    moves = [
        pltpu.make_async_copy(w_ref.at[pl.ds(k * patch, patch)], load_ref.at[k - 1], sem.at[k - 1])
        for k in range(1, channels)
    ]
    for move in moves:
        move.start()
    picked = edge_rows(steps * rows, cols, even_column())
    t_ref[:count] = g_ref[...]
    t_ref[count:] = exact(picked, beside_ref[...]) + edge_ref[...]
    table = fold_matrix(cols)
    frames, _ = f_ref.shape[1:3]
    height, width = SS * rows, SS * cols
    entries = KT * KS
    tiles = count // 128
    lane = lax.broadcasted_iota(jnp.int32, (entries, 128), 1)
    f_ref[...] = jnp.zeros_like(f_ref)
    for ch in range(channels):
        if ch:
            moves[ch - 1].wait()
        p = lax.dot_general(
            first_ref[...] if ch == 0 else load_ref[ch - 1],
            t_ref[...],
            (((1,), (1,)), ((), ())),
            preferred_element_type=jnp.float32,
        )
        for k in range(tiles):
            p_ref[ch, k] = p[:, k * 128 : (k + 1) * 128]
        p_ref[ch, tiles, :, :16] = p[:, count:]
        strided = lambda k, e: p_ref.at[ch, k][pl.ds(e, entries, stride=KS), :]
        by_e = [[strided(k, e) for k in range(tiles)] for e in range(KS)]
        by_e = [jnp.concatenate(v, axis=1) if tiles > 1 else v[0] for v in by_e]
        groups = steps * rows
        left = [strided(tiles, KS - LAP + k) for k in range(LAP)]
        right = [strided(tiles, k) for k in range(LAP)]
        for t in range(steps):
            for i in range(rows):
                ti = t * rows + i
                edge = jnp.zeros((entries, 128), jnp.float32)
                for k in range(LAP):
                    for v, src, dst in ((left[k], ti, k), (right[k], groups + ti, 128 - LAP + k)):
                        v = v if src == dst else pltpu.roll(v, (dst - src) % 128, 1)
                        edge = jnp.where(lane == dst, v, edge)
                q = jnp.concatenate([v[:, ti * cols : (ti + 1) * cols] for v in by_e] + [edge], axis=1)
                for a in range(KT):
                    f = ST * t + a - 1
                    if 0 <= f < ST * steps:
                        top = 8 - LAP + SS * i
                        f_ref[ch, f, top : top + KS, :] += q[a * KS : (a + 1) * KS]
    per = frames // parts
    me = lax.axis_index("mp")
    depth = KS * cols

    def folded(v):
        high = v[:, :depth].astype(jnp.bfloat16)
        low = (v[:, :depth] - high.astype(jnp.float32)).astype(jnp.bfloat16)
        both = jnp.dot(jnp.concatenate([high, low], axis=0), table, preferred_element_type=jnp.float32)
        out = both[: v.shape[0]] + both[v.shape[0] :]
        edge = v[:, depth:]
        at = lax.broadcasted_iota(jnp.int32, edge.shape, 1)
        first = out[:, :128] + jnp.where(at < LAP, edge, 0.0)
        last = out[:, width - 128 :] + jnp.where(at >= 128 - LAP, edge, 0.0)
        return jnp.concatenate([first, out[:, 128 : width - 128], last], axis=1)

    inner = f_ref[:, :, 8 : 8 + height].reshape(channels * frames * height, depth + 128)
    inner = folded(inner).reshape(channels, frames, height, width)
    for g in range(parts):
        block = inner[:, g * per : (g + 1) * per]

        @pl.when(me == g)
        def _():
            keep_ref[...] = block

        for s in range(1, parts):

            @pl.when(lax.rem(me + s, parts) == g)
            def _():
                send_ref[s - 1] = block

    above = f_ref[:, :, 0:8].reshape(channels * frames * 8, depth + 128)
    below = f_ref[:, :, 8 + height : 16 + height].reshape(channels * frames * 8, depth + 128)
    unrolled = lambda v: folded(v).reshape(channels, frames, 8, width)
    if split == 2:
        up = lax.axis_index("row") != 0
        rim = unrolled(jnp.where(up, above, below))
        halos[0][...] = jnp.where(up, rim[:, :, 8 - LAP :], rim[:, :, :LAP])
    else:
        halos[0][...] = unrolled(above)[:, :, 8 - LAP :]
        halos[1][...] = unrolled(below)[:, :, :LAP]


def video_partials(first, weight, flat, beside, edge, dims, channels):
    steps, rows, cols, parts, split = dims
    half = weight.shape[1]
    patch = weight.shape[0] // channels
    frames = ST * steps
    per = frames // parts
    height, width = SS * rows, SS * cols
    sides = 1 if split == 2 else 2
    f32 = lambda *shape: jax.ShapeDtypeStruct(shape, jnp.float32)
    return call(
        functools.partial(video_kernel, dims),
        (first, outside(weight), flat, beside, edge),
        [f32(channels, per, height, width), f32(parts - 1, channels, per, height, width)]
        + [f32(channels, frames, LAP, width)] * sides,
        20,
        scratch=[
            VMEM((channels, flat.shape[0] // 128 + 1, patch, 128), jnp.float32),
            VMEM((channels, frames, height + 16, KS * cols + 128), jnp.float32),
            VMEM((flat.shape[0] + 16, half), flat.dtype),
            VMEM((channels - 1, patch, half), flat.dtype),
            pltpu.SemaphoreType.DMA((channels - 1,)),
        ],
        hbm=(1,),
        flops=4 * weight.size * flat.shape[0],
    )


def rim_kernel(dims, keep_ref, send_ref, *refs):
    parts, split = dims
    rims, (keep_out, send_out) = refs[:-2], refs[-2:]
    per, height = keep_ref.shape[1:3]
    me, row = lax.axis_index("mp"), lax.axis_index("row")
    for s in range(parts):
        src = keep_ref if s == 0 else send_ref.at[s - 1]
        out = keep_out if s == 0 else send_out.at[s - 1]
        out[...] = src[...]
        at = pl.ds(lax.rem(me + s, parts) * per, per)
        if split == 2:

            @pl.when(row == 1)
            def _():
                out[:, :, :LAP] += rims[0][:, at]

            @pl.when(row == 0)
            def _():
                out[:, :, height - LAP :] += rims[0][:, at]
        else:
            out[:, :, :LAP] += rims[0][:, at]
            out[:, :, height - LAP :] += rims[1][:, at]


def unfold_kernel(dims, offsets, slab_ref, spread_ref, a_ref):
    groups, cols, touched = dims
    nr, nc = lax.axis_size("row"), lax.axis_size("col")
    me = lax.axis_index("col")
    width = SS * cols
    places = slab_ref.shape[1]
    lane = lax.broadcasted_iota(jnp.int32, (places, 128), 1)
    order = [jnp.bitwise_xor(me, o + h) for h in range(2) for o in offsets]
    wide = []
    for c in order:
        mine = slab_ref[c]
        before = slab_ref[jnp.maximum(c - 1, 0)][:, width - 128 :].astype(jnp.float32)
        after = slab_ref[jnp.minimum(c + 1, nc - 1)][:, :128].astype(jnp.float32)
        mixed = jnp.where((lane >= 128 - LAP) & (c > 0), before, 0.0)
        mixed = jnp.where((lane < LAP) & (c < nc - 1), after, mixed)
        wide.append(jnp.concatenate([mine, mixed.astype(mine.dtype)], axis=1))
    flat = jnp.dot(jnp.concatenate(wide, axis=0), unfold_matrix(cols), preferred_element_type=jnp.float32)
    u = [
        jnp.dot(
            spread_ref[...],
            flat[k * places : (k + 1) * places].astype(jnp.bfloat16),
            preferred_element_type=jnp.float32,
        )
        for k in range(nc)
    ]
    pack = 128 // cols
    step = 2
    while step * touched % 16:
        step *= 2
    for cg in range(nc // pack):
        for e in range(0, KS, step):
            some = [
                jnp.concatenate(
                    [
                        u[cg * pack + c][:, (e + d) * cols : (e + d + 1) * cols]
                        for c in range(pack)
                    ],
                    axis=1,
                )
                for d in range(step)
            ]
            for ti in range(groups):
                lanes = slice(ti * nc * cols + cg * 128, ti * nc * cols + (cg + 1) * 128)
                for r in range(nr):
                    at = (ti * nr + r) * touched
                    both = jnp.concatenate([v[at : at + touched] for v in some], axis=0)
                    a_ref[r, e * touched : (e + step) * touched, lanes] = both.astype(a_ref.dtype)


def weight_kernel(dims, s, a_ref, *refs):
    groups, cols, touched = dims
    pieces, (out_ref, m_ref) = refs[:-2], refs[-2:]
    half = out_ref.shape[1]
    tokens = []
    for ti in range(groups):
        for ref in pieces:
            tokens.append(ref[:, ti * cols : (ti + 1) * cols, :].reshape(-1, half))
    owner = lax.rem(lax.axis_index("row") + s, lax.axis_size("row"))
    m = jnp.dot(a_ref[owner], jnp.concatenate(tokens, axis=0), preferred_element_type=jnp.float32)
    for k in range(m_ref.shape[0]):
        for e in range(KS):
            m_ref.at[k][pl.ds(e, touched, stride=KS), :] = m[e * touched : (e + 1) * touched, k * 128 : (k + 1) * 128]
        out_ref[:, k * 128 : (k + 1) * 128] = m_ref[k]


def joined(parts):
    return parts[0] if len(parts) == 1 else jnp.concatenate(parts, axis=0)


def outside(x):
    return pltpu.with_memory_space_constraint(x, pltpu.HBM)


def call(kernel, args, outs, mib, scratch=(), hbm=(), out_hbm=(), flops=1 << 20):
    space = lambda k, hbm: pltpu.HBM if k in hbm else VMEM
    return pl.pallas_call(
        kernel,
        in_specs=[pl.BlockSpec(memory_space=space(k, hbm)) for k in range(len(args))],
        out_specs=[pl.BlockSpec(memory_space=space(k, out_hbm)) for k in range(len(outs))],
        out_shape=outs,
        scratch_shapes=scratch,
        cost_estimate=pl.CostEstimate(flops=flops, bytes_accessed=1 << 20, transcendentals=0),
        compiler_params=grant(mib),
    )(*args)


def both_gradients(video, grad_tokens, weight):
    steps, rows, cols, half = grad_tokens.shape
    channels, frames, height, width = video.shape
    patch = weight.shape[0]
    nr, nc, nm = lax.axis_size("row"), lax.axis_size("col"), lax.axis_size("mp")
    r, c = lax.axis_index("row"), lax.axis_index("col")
    groups = steps * rows
    count = groups * cols
    flat = grad_tokens.reshape(count, half)
    pixels = video.reshape(-1, width)
    dims = (steps, rows, cols, nm, nr)
    images = channels * frames
    lap = halo_rows(channels, frames)
    block = patch // (nr * nc)
    touched = max((k * block % KS + block + KS - 1) // KS for k in range(nr * nc))
    units = nr * touched
    bf16 = lambda *shape: jax.ShapeDtypeStruct(shape, video.dtype)
    f32 = lambda *shape: jax.ShapeDtypeStruct(shape, jnp.float32)

    table, spread = row_tables(channels, frames, height, steps, rows, nr, nc, block, touched)
    places = table.shape[1]
    pixels, tokens, table, spread, edge, *halos = call(
        functools.partial(prep_kernel, (nr, images, height, groups, cols)),
        (outside(pixels), outside(flat), outside(table), outside(spread)),
        [bf16(*x.shape) for x in (pixels, flat, table)] + [bf16(*spread.shape[1:]), bf16(16, half)]
        + [bf16(lap, width)] * (1 if nr == 2 else 2),
        6,
        scratch=[pltpu.SemaphoreType.DMA((4,))],
        hbm=(0, 1, 2, 3),
    )
    if nr == 2:
        halos = [swap(halos[0], "row", 1)]
    else:
        halos = [shift(halos[1], "row", 1), shift(halos[0], "row", -1)]

    slabs, first = call(
        functools.partial(slab_kernel, nr),
        (table, pixels, outside(weight), *halos),
        [pltpu.HBM((nc, places, width), video.dtype), bf16(patch // channels, half)],
        12,
        scratch=[
            VMEM((table.shape[2], width), video.dtype),
            VMEM((nc, places, width), video.dtype),
            pltpu.SemaphoreType.DMA((nc + 1,)),
        ],
        hbm=(2,),
        out_hbm=(0,),
        flops=2 * table.size * width,
    )
    slabs = lax.all_to_all(slabs, "col", 0, 0, tiled=True)

    beside = swap(tokens, "col", 1)
    ring = [(i + d, i + 1 - d) for i in range(1, nc - 1, 2) for d in range(2)]
    edge = lax.ppermute(edge, "col", ring)

    held, offsets = [tokens[None]], [2 * k for k in range(nc // 2)]
    for bit in offsets[1:]:
        held.append(swap(tokens[None], "col", bit))
    others = [beside[None], swap(joined(held[1:]), "col", 1)]
    pieces = held + others

    keep, send, *rims = video_partials(first, weight, tokens, beside, edge, dims, channels)
    if nr == 2:
        rims = [swap(rims[0], "row", 1)]
    else:
        rims = [shift(rims[1], "row", 1), shift(rims[0], "row", -1)]
    keep, send = call(
        functools.partial(rim_kernel, (nm, nr)),
        (keep, send, *rims),
        [f32(*keep.shape), f32(*send.shape)],
        6,
    )
    video_grad = keep
    for s in range(1, nm):
        part = rotate(send[s - 1], "mp", s)
        video_grad = video_grad + part

    share = touched * KS
    (unfolded,) = call(
        functools.partial(unfold_kernel, (groups, cols, touched), tuple(offsets)),
        (slabs, spread),
        [bf16(nr, share, groups * nc * cols)],
        10,
        flops=2 * nc * groups * units * (width + 128) * KS * cols,
    )
    sums = [None] * nr
    for s in (*range(1, nr), 0):
        (mine,) = call(
            functools.partial(weight_kernel, (groups, cols, touched), s),
            (unfolded, *pieces),
            [f32(share, half)],
            8,
            scratch=[VMEM((half // 128, share, 128), jnp.float32)],
            flops=2 * share * groups * nc * cols * half,
        )
        if block % KS:
            mine = lax.dynamic_slice_in_dim(mine, ((r + s) % nr * nc + c) * block % KS, block, 0)
        sums[s] = rotate(mine, "row", s) if s else mine
    total = functools.reduce(jnp.add, sums)
    weight_grad = total * lax.rsqrt(jnp.float32(count * nr * nc))
    return video_grad, weight_grad


def solution(mesh):
    return jax.shard_map(
        both_gradients,
        mesh=mesh,
        in_specs=(P(None, None, "row", "col"), P(None, "row", "col", "mp"), P(None, "mp")),
        out_specs=(P(None, "mp", "row", "col"), P(("row", "col"), "mp")),
        check_vma=False,
    )
```

profile of v0, /device:TPU:14, one launch (start us, length us, event | category | flops | bytes accessed | tf_op | source)
XLA Modules:
  0.0 69.0 jit_solution(17933013422637124754)
XLA Ops:
  0.6 1.2 %shard_map.68 = (bf16[288,384]{1,0:T(8,128)(2,1)S(1)}, bf16[128,512]{1,0:T(8,128)(2,1)S(1)}, bf16[8,72,352]{2,1,0:T(8,128)(2,1)S(1)}, bf16[96,72]{1,0:T(8,128)(2...) custom-call(bf16[288,384]{1,0:T(8,128)(2,1)} %bitcast.13, bf16[128,512]{1,0:T(8,128)(2,1)} %bitcast.14, ...), custom_call_target="tpu_custom_call" | custom-call | flops 1048576 | bytes 1048576 | tf_op jit(solution)/shard_map/pallas_call | solution.py:390
  2.0 1.2 %collective-permute-done.refs_0_ = bf16[32,384]{1,0:T(8,128)(2,1)S(1)} collective-permute-done((bf16[32,384]{1,0:T(8,128)(2,1)S(1)}, bf16[32,384]{1,0:T(8,128)(2,1)S(1)}, u32[]{:S(2)}, u32[]{:S(2)}) %collective-permute-start) | collective-permute-done | bytes 24608 | tf_op jit(solution)/shard_map/ppermute | solution.py:23
  3.1 1.4 %shard_map.69 = (bf16[8,72,384]{2,1,0:T(8,128)(2,1)}, bf16[1024,512]{1,0:T(8,128)(2,1)S(1)}) custom-call(bf16[8,72,352]{2,1,0:T(8,128)(2,1)S(1)} %get-tuple-element.15.table_ref, bf16[288,384]{1,0:T(8,128)(2,1)S(1)} %get-tuple-element.16.video_ref, bf16[3072,512]{1,0:T(8,128)(2,1)} %w_ref.1, bf16[32,384]{1,0:T(8,128)(2,1)S(1)} %collective-permute-done.refs_0_), custom_call_target="tpu_custom_call" | custom-call | flops 155713536 | bytes 1048576 | tf_op jit(solution)/shard_map/pallas_call | solution.py:390
  4.5 6.2 %all-to-all-start = ((bf16[8,72,384]{2,1,0:T(8,128)(2,1)}), bf16[8,72,384]{2,1,0:T(8,128)(2,1)S(1)}, u32[]{:S(2)}, u32[]{:S(2)}) async-start(bf16[8,72,384]{2,1,0:T(8,128)(2,1)} %get-tuple-element.26), calls=%async_computation | async-start | bytes 884736 | tf_op jit(solution)/shard_map/all_to_all | solution.py:450
  10.8 0.6 collective-permute-start.5
  11.3 2.4 %collective-permute-start.6 = (bf16[1,128,512]{2,1,0:T(8,128)(2,1)S(1)}, bf16[1,128,512]{2,1,0:T(8,128)(2,1)S(1)}, u32[]{:S(2)}, u32[]{:S(2)}) collective-permute-start(bf16[1,128,512]{2,1,0:T(8,128)(2,1)S(1)} %bitcast.6), channel_id=1, source_target_pairs={{0,8},{2,10},{4,12},{6,14},{8,0},{10,2},{12,4},{14,6},{1,9},{3,11}... | collective-permute-start | bytes 393224 | tf_op jit(solution)/shard_map/ppermute | solution.py:23
  13.7 0.6 collective-permute-start.7
  14.2 8.8 %collective-permute-done.5.refs_1_ = bf16[1,128,512]{2,1,0:T(8,128)(2,1)S(1)} collective-permute-done((bf16[1,128,512]{2,1,0:T(8,128)(2,1)S(1)}, bf16[1,128,512]{2,1,0:T(8,128)(2,1)S(1)}, u32[]{:S(2)}, u32[]{:S(2)}) %collective-permute-start.5) | collective-permute-done | bytes 131104 | tf_op jit(solution)/shard_map/ppermute | solution.py:23
  23.0 5.9 %collective-permute-done.6.refs_2_ = bf16[1,128,512]{2,1,0:T(8,128)(2,1)S(1)} collective-permute-done((bf16[1,128,512]{2,1,0:T(8,128)(2,1)S(1)}, bf16[1,128,512]{2,1,0:T(8,128)(2,1)S(1)}, u32[]{:S(2)}, u32[]{:S(2)}) %collective-permute-start.6) | collective-permute-done | bytes 131104 | tf_op jit(solution)/shard_map/ppermute | solution.py:23
  29.0 4.6 %collective-permute-done.7.refs_3_ = bf16[1,128,512]{2,1,0:T(8,128)(2,1)S(1)} collective-permute-done((bf16[1,128,512]{2,1,0:T(8,128)(2,1)S(1)}, bf16[1,128,512]{2,1,0:T(8,128)(2,1)S(1)}, u32[]{:S(2)}, u32[]{:S(2)}) %collective-permute-start.7) | collective-permute-done | bytes 131104 | tf_op jit(solution)/shard_map/ppermute | solution.py:23
  33.6 0.6 collective-permute-start.8
  34.3 1.5 %collective-permute-start.1 = (bf16[128,512]{1,0:T(8,128)(2,1)S(1)}, bf16[128,512]{1,0:T(8,128)(2,1)S(1)}, u32[]{:S(2)}, u32[]{:S(2)}) collective-permute-start(bf16[128,512]{1,0:T(8,128)(2,1)S(1)} %get-tuple-element.19.g_ref), channel_id=1, source_target_pairs={{0,2},{2,0},{4,6},{6,4},{8,10},{10,8},{12,14},{14,12},{1,3},{3,1},... | collective-permute-start | bytes 393224 | tf_op jit(solution)/shard_map/ppermute | solution.py:23
  35.7 1.2 %shard_map.72.a_ref = bf16[2,192,1024]{2,1,0:T(8,128)(2,1)S(1)} custom-call(bf16[8,72,384]{2,1,0:T(8,128)(2,1)S(1)} %all-to-all-done.slab_ref, bf16[96,72]{1,0:T(8,128)(2,1)S(1)} %get-tuple-element.27.spread_ref), custom_call_target="tpu_custom_call" | custom-call | flops 402653184 | bytes 1048576 | tf_op jit(solution)/shard_map/pallas_call | solution.py:390
  37.0 9.7 %collective-permute-done.1.beside_ref = bf16[128,512]{1,0:T(8,128)(2,1)S(1)} collective-permute-done((bf16[128,512]{1,0:T(8,128)(2,1)S(1)}, bf16[128,512]{1,0:T(8,128)(2,1)S(1)}, u32[]{:S(2)}, u32[]{:S(2)}) %collective-permute-start.1) | collective-permute-done | bytes 131104 | tf_op jit(solution)/shard_map/ppermute | solution.py:23
  46.7 0.5 shard_map.74
  47.3 3.1 %collective-permute-start.2 = (bf16[16,512]{1,0:T(8,128)(2,1)S(1)}, bf16[16,512]{1,0:T(8,128)(2,1)S(1)}, u32[]{:S(2)}, u32[]{:S(2)}) collective-permute-start(bf16[16,512]{1,0:T(8,128)(2,1)S(1)} %get-tuple-element.20), channel_id=1, source_target_pairs={{2,4},{4,2},{6,8},{8,6},{10,12},{12,10},{3,5},{5,3},{7,9},{9,7},{1... | collective-permute-start | bytes 49160 | tf_op jit(solution)/shard_map/ppermute | solution.py:454
  50.4 3.4 %collective-permute-done.2.edge_ref = bf16[16,512]{1,0:T(8,128)(2,1)S(1)} collective-permute-done((bf16[16,512]{1,0:T(8,128)(2,1)S(1)}, bf16[16,512]{1,0:T(8,128)(2,1)S(1)}, u32[]{:S(2)}, u32[]{:S(2)}) %collective-permute-start.2) | collective-permute-done | bytes 16416 | tf_op jit(solution)/shard_map/ppermute | solution.py:454
  53.8 4.2 %shard_map.70 = (f32[3,2,24,384]{3,2,1,0:T(8,128)S(1)}, f32[1,3,2,24,384]{4,3,2,1,0:T(8,128)S(1)}, f32[3,4,2,384]{3,2,1,0:T(2,128)S(1)}) custom-call(bf16[1024,512]{1,0:T(8,128)(2,1)S(1)} %get-tuple-element.18.first_ref, bf16[3072,512]{1,0:T(8,128)(2,1)} %w_ref.1, bf16[128,512]{1,0:T(8,128)(2,1)S(1)} %get-tuple-element.19.g_ref, ...), custom_call_target="tpu_custom_call" | custom-call | flops 805306368 | bytes 1048576 | tf_op jit(solution)/shard_map/pallas_call | solution.py:390
  58.1 1.2 %collective-permute-done.3.refs_0_ = f32[3,4,2,384]{3,2,1,0:T(2,128)S(1)} collective-permute-done((f32[3,4,2,384]{3,2,1,0:T(2,128)S(1)}, f32[3,4,2,384]{3,2,1,0:T(2,128)S(1)}, u32[]{:S(2)}, u32[]{:S(2)}) %collective-permute-start.3) | collective-permute-done | bytes 36896 | tf_op jit(solution)/shard_map/ppermute | solution.py:23
  59.4 0.6 collective-permute-start.4
  59.9 7.0 %collective-permute-done.4 = f32[3,2,24,384]{3,2,1,0:T(8,128)S(1)} collective-permute-done((f32[3,2,24,384]{3,2,1,0:T(8,128)S(1)}, f32[3,2,24,384]{3,2,1,0:T(8,128)S(1)}, u32[]{:S(2)}, u32[]{:S(2)}) %collective-permute-start.4) | collective-permute-done | bytes 221216 | tf_op jit(solution)/shard_map/ppermute | solution.py:33
  66.9 0.7 %add.6 = f32[3,2,24,384]{3,2,1,0:T(8,128)} add(f32[3,2,24,384]{3,2,1,0:T(8,128)S(1)} %get-tuple-element.24, f32[3,2,24,384]{3,2,1,0:T(8,128)S(1)} %collective-permute-done.4) | non-fusion elementwise | flops 55296 | bytes 663552 | tf_op jit(solution)/shard_map/add | solution.py:476
  67.6 0.5 shard_map.73
  68.2 0.8 %add_multiply_fusion = f32[192,512]{1,0:T(8,128)} fusion(f32[192,512]{1,0:T(8,128)S(1)} %shard_map.73, f32[192,512]{1,0:T(8,128)S(1)} %collective-permute-done.9), kind=kLoop, calls=%fused_computation.1 | loop fusion | flops 196608 | bytes 1179648 | tf_op jit(solution)/shard_map/mul | solution.py:500
  (8 shorter events, 0.3 us)
Async XLA Ops:
  1.9 1.3 %collective-permute-start = (bf16[32,384]{1,0:T(8,128)(2,1)S(1)}, bf16[32,384]{1,0:T(8,128)(2,1)S(1)}, u32[]{:S(2)}, u32[]{:S(2)}) collective-permute-start(bf16[32,384]{1,0:T(8,128)(2,1)S(1)} %get-tuple-element.17), channel_id=1, source_target_pairs={{0,16},{16,0},{1,17},{17,1},{2,18},{18,2},{3,19},{19,3},{4,20},{20... | collective-permute-start | bytes 73736 | tf_op jit(solution)/shard_map/ppermute | solution.py:23
  4.5 31.2 %all-to-all-start = ((bf16[8,72,384]{2,1,0:T(8,128)(2,1)}), bf16[8,72,384]{2,1,0:T(8,128)(2,1)S(1)}, u32[]{:S(2)}, u32[]{:S(2)}) async-start(bf16[8,72,384]{2,1,0:T(8,128)(2,1)} %get-tuple-element.26), calls=%async_computation | async-start | bytes 884736 | tf_op jit(solution)/shard_map/all_to_all | solution.py:450
  10.8 12.3 %collective-permute-start.5 = (bf16[1,128,512]{2,1,0:T(8,128)(2,1)S(1)}, bf16[1,128,512]{2,1,0:T(8,128)(2,1)S(1)}, u32[]{:S(2)}, u32[]{:S(2)}) collective-permute-start(bf16[1,128,512]{2,1,0:T(8,128)(2,1)S(1)} %bitcast.5), channel_id=1, source_target_pairs={{0,4},{2,6},{4,0},{6,2},{8,12},{10,14},{12,8},{14,10},{1,5},{3,7},... | collective-permute-start | bytes 393224 | tf_op jit(solution)/shard_map/ppermute | solution.py:23
  11.3 17.6 %collective-permute-start.6 = (bf16[1,128,512]{2,1,0:T(8,128)(2,1)S(1)}, bf16[1,128,512]{2,1,0:T(8,128)(2,1)S(1)}, u32[]{:S(2)}, u32[]{:S(2)}) collective-permute-start(bf16[1,128,512]{2,1,0:T(8,128)(2,1)S(1)} %bitcast.6), channel_id=1, source_target_pairs={{0,8},{2,10},{4,12},{6,14},{8,0},{10,2},{12,4},{14,6},{1,9},{3,11}... | collective-permute-start | bytes 393224 | tf_op jit(solution)/shard_map/ppermute | solution.py:23
  13.7 19.9 %collective-permute-start.7 = (bf16[1,128,512]{2,1,0:T(8,128)(2,1)S(1)}, bf16[1,128,512]{2,1,0:T(8,128)(2,1)S(1)}, u32[]{:S(2)}, u32[]{:S(2)}) collective-permute-start(bf16[1,128,512]{2,1,0:T(8,128)(2,1)S(1)} %bitcast.7), channel_id=1, source_target_pairs={{0,12},{2,14},{4,8},{6,10},{8,4},{10,6},{12,0},{14,2},{1,13},{3,15... | collective-permute-start | bytes 393224 | tf_op jit(solution)/shard_map/ppermute | solution.py:23
  33.6 13.0 %collective-permute-start.8 = (bf16[3,128,512]{2,1,0:T(8,128)(2,1)S(1)}, bf16[3,128,512]{2,1,0:T(8,128)(2,1)S(1)}, u32[]{:S(2)}, u32[]{:S(2)}) collective-permute-start(bf16[3,128,512]{2,1,0:T(8,128)(2,1)S(1)} %pad_maximum_fusion), channel_id=1, source_target_pairs={{0,2},{2,0},{4,6},{6,4},{8,10},{10,8},{12,14},{14,12},{1,3},{3,1},... | collective-permute-start | bytes 1179656 | tf_op jit(solution)/shard_map/ppermute | solution.py:23
  34.3 12.4 %collective-permute-start.1 = (bf16[128,512]{1,0:T(8,128)(2,1)S(1)}, bf16[128,512]{1,0:T(8,128)(2,1)S(1)}, u32[]{:S(2)}, u32[]{:S(2)}) collective-permute-start(bf16[128,512]{1,0:T(8,128)(2,1)S(1)} %get-tuple-element.19.g_ref), channel_id=1, source_target_pairs={{0,2},{2,0},{4,6},{6,4},{8,10},{10,8},{12,14},{14,12},{1,3},{3,1},... | collective-permute-start | bytes 393224 | tf_op jit(solution)/shard_map/ppermute | solution.py:23
  47.2 21.0 %collective-permute-start.9 = (f32[192,512]{1,0:T(8,128)S(1)}, f32[192,512]{1,0:T(8,128)S(1)}, u32[]{:S(2)}, u32[]{:S(2)}) collective-permute-start(f32[192,512]{1,0:T(8,128)S(1)} %shard_map.74), channel_id=1, source_target_pairs={{0,16},{16,0},{1,17},{17,1},{2,18},{18,2},{3,19},{19,3},{4,20},{20... | collective-permute-start | bytes 1179656 | tf_op jit(solution)/shard_map/ppermute | solution.py:33
  47.3 6.5 %collective-permute-start.2 = (bf16[16,512]{1,0:T(8,128)(2,1)S(1)}, bf16[16,512]{1,0:T(8,128)(2,1)S(1)}, u32[]{:S(2)}, u32[]{:S(2)}) collective-permute-start(bf16[16,512]{1,0:T(8,128)(2,1)S(1)} %get-tuple-element.20), channel_id=1, source_target_pairs={{2,4},{4,2},{6,8},{8,6},{10,12},{12,10},{3,5},{5,3},{7,9},{9,7},{1... | collective-permute-start | bytes 49160 | tf_op jit(solution)/shard_map/ppermute | solution.py:454
  58.0 1.3 %collective-permute-start.3 = (f32[3,4,2,384]{3,2,1,0:T(2,128)S(1)}, f32[3,4,2,384]{3,2,1,0:T(2,128)S(1)}, u32[]{:S(2)}, u32[]{:S(2)}) collective-permute-start(f32[3,4,2,384]{3,2,1,0:T(2,128)S(1)} %get-tuple-element.23), channel_id=1, source_target_pairs={{0,16},{16,0},{1,17},{17,1},{2,18},{18,2},{3,19},{19,3},{4,20},{20... | collective-permute-start | bytes 110600 | tf_op jit(solution)/shard_map/ppermute | solution.py:23
  59.4 7.6 %collective-permute-start.4 = (f32[3,2,24,384]{3,2,1,0:T(8,128)S(1)}, f32[3,2,24,384]{3,2,1,0:T(8,128)S(1)}, u32[]{:S(2)}, u32[]{:S(2)}) collective-permute-start(f32[3,2,24,384]{3,2,1,0:T(8,128)S(1)} %bitcast.12), channel_id=1, source_target_pairs={{0,1},{1,0},{2,3},{3,2},{4,5},{5,4},{6,7},{7,6},{8,9},{9,8},{10,11... | collective-permute-start | bytes 663560 | tf_op jit(solution)/shard_map/ppermute | solution.py:33
where the time goes:
time: 69.3 us; the launch traced here: 69 us
  waiting for transfers between devices  41.8 us (60%)
  starting transfers between devices  15.7 us (23%)
  Pallas kernels  9.14 us (13%)
  other arithmetic  1.57 us (2%)
  between operations  0.73 us (1%)
    ppermute x7, waiting for transfers between devices, swap(): return lax.ppermute(x, axis, [(i, i ^ bit) for i in range(n)])  31.4 us
    pallas_call x7, Pallas kernels, call(): pl.pallas_call(kernel, in_specs=[pl.BlockSpec(memory_space=space(k, hbm))...  9.14 us
    ppermute x2, waiting for transfers between devices, rotate(): return lax.ppermute(x, axis, [(i, (i + by) % n) for i in range(n)])  7 us
    all_to_all x1, starting transfers between devices, both_gradients(): slabs = lax.all_to_all(slabs, 'col', 0, 0, tiled=True)  6.23 us
    ppermute x7, starting transfers between devices, swap(): return lax.ppermute(x, axis, [(i, i ^ bit) for i in range(n)])  5.72 us
    ppermute x1, waiting for transfers between devices, both_gradients(): edge = lax.ppermute(edge, 'col', ring)  3.43 us
    ppermute x1, starting transfers between devices, both_gradients(): edge = lax.ppermute(edge, 'col', ring)  3.1 us
  transfers between devices with their start and end apart: 11, of which 8 were waited for; matrix products, arithmetic and copies ran while one was open for 1% of the time, Pallas kernels for 9%

commit v1 on v0

--- a/solution.py
+++ b/solution.py
@@ -179,7 +179,7 @@
         move.start()
     picked = edge_rows(steps * rows, cols, even_column())
     t_ref[:count] = g_ref[...]
-    t_ref[count:] = exact(picked, beside_ref[...]) + edge_ref[...]
+    t_ref[count:] = exact(picked, beside_ref[0]) + edge_ref[...]
     table = fold_matrix(cols)
     frames, _ = f_ref.shape[1:3]
     height, width = SS * rows, SS * cols
@@ -449,14 +449,13 @@
     )
     slabs = lax.all_to_all(slabs, "col", 0, 0, tiled=True)
 
-    beside = swap(tokens, "col", 1)
     ring = [(i + d, i + 1 - d) for i in range(1, nc - 1, 2) for d in range(2)]
     edge = lax.ppermute(edge, "col", ring)
-
     held, offsets = [tokens[None]], [2 * k for k in range(nc // 2)]
     for bit in offsets[1:]:
         held.append(swap(tokens[None], "col", bit))
-    others = [beside[None], swap(joined(held[1:]), "col", 1)]
+    beside = swap(joined(held[:2]), "col", 1)
+    others = [beside, swap(joined(held[2:]), "col", 1)]
     pieces = held + others
 
     keep, send, *rims = video_partials(first, weight, tokens, beside, edge, dims, channels)

time: 69.3 us -> 63.6 us (0.918)
  waiting for transfers between devices: 41.8 us -> 37.6 us
  starting transfers between devices: 15.7 us -> 14.3 us
    ppermute x7, waiting for transfers between devices: 31.4 us -> 27.1 us  [swap(): return lax.ppermute(x, axis, [(i, i ^ bit) for i in range(n)])]
    ppermute x7, starting transfers between devices: 5.72 us -> 4.33 us  [swap(): return lax.ppermute(x, axis, [(i, i ^ bit) for i in range(n)])]
where the time goes in v1:
time: 63.6 us; the launch traced here: 63.3 us
  waiting for transfers between devices  37.6 us (59%)
  starting transfers between devices  14.3 us (22%)
  Pallas kernels  9.14 us (14%)
  other arithmetic  1.58 us (2%)
  between operations  0.75 us (1%)
    ppermute x7, waiting for transfers between devices, swap(): return lax.ppermute(x, axis, [(i, i ^ bit) for i in range(n)])  27.1 us
    pallas_call x7, Pallas kernels, call(): pl.pallas_call(kernel, in_specs=[pl.BlockSpec(memory_space=space(k, hbm))...  9.14 us
    ppermute x2, waiting for transfers between devices, rotate(): return lax.ppermute(x, axis, [(i, (i + by) % n) for i in range(n)])  7 us
    all_to_all x1, starting transfers between devices, both_gradients(): slabs = lax.all_to_all(slabs, 'col', 0, 0, tiled=True)  6.23 us
    ppermute x7, starting transfers between devices, swap(): return lax.ppermute(x, axis, [(i, i ^ bit) for i in range(n)])  4.33 us
    ppermute x1, waiting for transfers between devices, both_gradients(): edge = lax.ppermute(edge, 'col', ring)  3.43 us
    ppermute x1, starting transfers between devices, both_gradients(): edge = lax.ppermute(edge, 'col', ring)  3.1 us
  transfers between devices with their start and end apart: 11, of which 8 were waited for; matrix products, arithmetic and copies ran while one was open for 1% of the time, Pallas kernels for 9%

profile of v1, /device:TPU:14, one launch (start us, length us, event | category | flops | bytes accessed | tf_op | source)
XLA Modules:
  0.0 63.3 jit_solution(5938385406090282177)
XLA Ops:
  0.6 1.2 %shard_map.68 = (bf16[288,384]{1,0:T(8,128)(2,1)S(1)}, bf16[128,512]{1,0:T(8,128)(2,1)S(1)}, bf16[8,72,352]{2,1,0:T(8,128)(2,1)S(1)}, bf16[96,72]{1,0:T(8,128)(2...) custom-call(bf16[288,384]{1,0:T(8,128)(2,1)} %bitcast.11, bf16[128,512]{1,0:T(8,128)(2,1)} %bitcast.12, ...), custom_call_target="tpu_custom_call" | custom-call | flops 1048576 | bytes 1048576 | tf_op jit(solution)/shard_map/pallas_call | solution.py:390
  1.9 0.1 collective-permute-start
  2.0 1.2 %collective-permute-done.refs_0_ = bf16[32,384]{1,0:T(8,128)(2,1)S(1)} collective-permute-done((bf16[32,384]{1,0:T(8,128)(2,1)S(1)}, bf16[32,384]{1,0:T(8,128)(2,1)S(1)}, u32[]{:S(2)}, u32[]{:S(2)}) %collective-permute-start) | collective-permute-done | bytes 24608 | tf_op jit(solution)/shard_map/ppermute | solution.py:23
  3.1 1.4 %shard_map.69 = (bf16[8,72,384]{2,1,0:T(8,128)(2,1)}, bf16[1024,512]{1,0:T(8,128)(2,1)S(1)}) custom-call(bf16[8,72,352]{2,1,0:T(8,128)(2,1)S(1)} %get-tuple-element.15.table_ref, bf16[288,384]{1,0:T(8,128)(2,1)S(1)} %get-tuple-element.16.video_ref, bf16[3072,512]{1,0:T(8,128)(2,1)} %w_ref.1, bf16[32,384]{1,0:T(8,128)(2,1)S(1)} %collective-permute-done.refs_0_), custom_call_target="tpu_custom_call" | custom-call | flops 155713536 | bytes 1048576 | tf_op jit(solution)/shard_map/pallas_call | solution.py:390
  4.5 6.2 %all-to-all-start = ((bf16[8,72,384]{2,1,0:T(8,128)(2,1)}), bf16[8,72,384]{2,1,0:T(8,128)(2,1)S(1)}, u32[]{:S(2)}, u32[]{:S(2)}) async-start(bf16[8,72,384]{2,1,0:T(8,128)(2,1)} %get-tuple-element.26), calls=%async_computation | async-start | bytes 884736 | tf_op jit(solution)/shard_map/all_to_all | solution.py:450
  10.8 0.6 collective-permute-start.1
  11.3 2.4 %collective-permute-start.6 = (bf16[1,128,512]{2,1,0:T(8,128)(2,1)S(1)}, bf16[1,128,512]{2,1,0:T(8,128)(2,1)S(1)}, u32[]{:S(2)}, u32[]{:S(2)}) collective-permute-start(bf16[1,128,512]{2,1,0:T(8,128)(2,1)S(1)} %bitcast.5), channel_id=1, source_target_pairs={{0,8},{2,10},{4,12},{6,14},{8,0},{10,2},{12,4},{14,6},{1,9},{3,11}... | collective-permute-start | bytes 393224 | tf_op jit(solution)/shard_map/ppermute | solution.py:23
  13.7 0.6 collective-permute-start.7
  14.2 8.8 %collective-permute-done.1.refs_1_ = bf16[1,128,512]{2,1,0:T(8,128)(2,1)S(1)} collective-permute-done((bf16[1,128,512]{2,1,0:T(8,128)(2,1)S(1)}, bf16[1,128,512]{2,1,0:T(8,128)(2,1)S(1)}, u32[]{:S(2)}, u32[]{:S(2)}) %collective-permute-start.1) | collective-permute-done | bytes 131104 | tf_op jit(solution)/shard_map/ppermute | solution.py:23
  23.1 5.8 %collective-permute-done.6.refs_2_ = bf16[1,128,512]{2,1,0:T(8,128)(2,1)S(1)} collective-permute-done((bf16[1,128,512]{2,1,0:T(8,128)(2,1)S(1)}, bf16[1,128,512]{2,1,0:T(8,128)(2,1)S(1)}, u32[]{:S(2)}, u32[]{:S(2)}) %collective-permute-start.6) | collective-permute-done | bytes 131104 | tf_op jit(solution)/shard_map/ppermute | solution.py:23
  29.0 4.6 %collective-permute-done.7.refs_3_ = bf16[1,128,512]{2,1,0:T(8,128)(2,1)S(1)} collective-permute-done((bf16[1,128,512]{2,1,0:T(8,128)(2,1)S(1)}, bf16[1,128,512]{2,1,0:T(8,128)(2,1)S(1)}, u32[]{:S(2)}, u32[]{:S(2)}) %collective-permute-start.7) | collective-permute-done | bytes 131104 | tf_op jit(solution)/shard_map/ppermute | solution.py:23
  33.6 0.6 collective-permute-start.8
  34.3 1.2 %shard_map.72.a_ref = bf16[2,192,1024]{2,1,0:T(8,128)(2,1)S(1)} custom-call(bf16[8,72,384]{2,1,0:T(8,128)(2,1)S(1)} %all-to-all-done.slab_ref, bf16[96,72]{1,0:T(8,128)(2,1)S(1)} %get-tuple-element.27.spread_ref), custom_call_target="tpu_custom_call" | custom-call | flops 402653184 | bytes 1048576 | tf_op jit(solution)/shard_map/pallas_call | solution.py:390
  35.5 5.5 %collective-permute-done.8.refs_5_ = bf16[2,128,512]{2,1,0:T(8,128)(2,1)S(1)} collective-permute-done((bf16[2,128,512]{2,1,0:T(8,128)(2,1)S(1)}, bf16[2,128,512]{2,1,0:T(8,128)(2,1)S(1)}, u32[]{:S(2)}, u32[]{:S(2)}) %collective-permute-start.8) | collective-permute-done | bytes 262176 | tf_op jit(solution)/shard_map/ppermute | solution.py:23
  41.0 0.5 shard_map.74
  41.6 3.1 %collective-permute-start.3 = (bf16[16,512]{1,0:T(8,128)(2,1)S(1)}, bf16[16,512]{1,0:T(8,128)(2,1)S(1)}, u32[]{:S(2)}, u32[]{:S(2)}) collective-permute-start(bf16[16,512]{1,0:T(8,128)(2,1)S(1)} %get-tuple-element.20), channel_id=1, source_target_pairs={{2,4},{4,2},{6,8},{8,6},{10,12},{12,10},{3,5},{5,3},{7,9},{9,7},{1... | collective-permute-start | bytes 49160 | tf_op jit(solution)/shard_map/ppermute | solution.py:453
  44.7 3.4 %collective-permute-done.3.edge_ref = bf16[16,512]{1,0:T(8,128)(2,1)S(1)} collective-permute-done((bf16[16,512]{1,0:T(8,128)(2,1)S(1)}, bf16[16,512]{1,0:T(8,128)(2,1)S(1)}, u32[]{:S(2)}, u32[]{:S(2)}) %collective-permute-start.3) | collective-permute-done | bytes 16416 | tf_op jit(solution)/shard_map/ppermute | solution.py:453
  48.2 4.2 %shard_map.70 = (f32[3,2,24,384]{3,2,1,0:T(8,128)S(1)}, f32[1,3,2,24,384]{4,3,2,1,0:T(8,128)S(1)}, f32[3,4,2,384]{3,2,1,0:T(2,128)S(1)}) custom-call(bf16[1024,512]{1,0:T(8,128)(2,1)S(1)} %get-tuple-element.18.first_ref, bf16[3072,512]{1,0:T(8,128)(2,1)} %w_ref.1, bf16[128,512]{1,0:T(8,128)(2,1)S(1)} %get-tuple-element.19.g_ref, ...), custom_call_target="tpu_custom_call" | custom-call | flops 805306368 | bytes 1048576 | tf_op jit(solution)/shard_map/pallas_call | solution.py:390
  52.4 1.2 %collective-permute-done.4.refs_0_ = f32[3,4,2,384]{3,2,1,0:T(2,128)S(1)} collective-permute-done((f32[3,4,2,384]{3,2,1,0:T(2,128)S(1)}, f32[3,4,2,384]{3,2,1,0:T(2,128)S(1)}, u32[]{:S(2)}, u32[]{:S(2)}) %collective-permute-start.4) | collective-permute-done | bytes 36896 | tf_op jit(solution)/shard_map/ppermute | solution.py:23
  53.7 0.6 collective-permute-start.5
  54.3 7.0 %collective-permute-done.5 = f32[3,2,24,384]{3,2,1,0:T(8,128)S(1)} collective-permute-done((f32[3,2,24,384]{3,2,1,0:T(8,128)S(1)}, f32[3,2,24,384]{3,2,1,0:T(8,128)S(1)}, u32[]{:S(2)}, u32[]{:S(2)}) %collective-permute-start.5) | collective-permute-done | bytes 221216 | tf_op jit(solution)/shard_map/ppermute | solution.py:33
  61.3 0.7 %add.6 = f32[3,2,24,384]{3,2,1,0:T(8,128)} add(f32[3,2,24,384]{3,2,1,0:T(8,128)S(1)} %get-tuple-element.24, f32[3,2,24,384]{3,2,1,0:T(8,128)S(1)} %collective-permute-done.5) | non-fusion elementwise | flops 55296 | bytes 663552 | tf_op jit(solution)/shard_map/add | solution.py:475
  62.0 0.5 shard_map.73
  62.5 0.8 %add_multiply_fusion = f32[192,512]{1,0:T(8,128)} fusion(f32[192,512]{1,0:T(8,128)S(1)} %shard_map.73, f32[192,512]{1,0:T(8,128)S(1)} %collective-permute-done.9), kind=kLoop, calls=%fused_computation | loop fusion | flops 196608 | bytes 1179648 | tf_op jit(solution)/shard_map/mul | solution.py:499
  (9 shorter events, 0.3 us)
Async XLA Ops:
  1.9 1.3 %collective-permute-start = (bf16[32,384]{1,0:T(8,128)(2,1)S(1)}, bf16[32,384]{1,0:T(8,128)(2,1)S(1)}, u32[]{:S(2)}, u32[]{:S(2)}) collective-permute-start(bf16[32,384]{1,0:T(8,128)(2,1)S(1)} %get-tuple-element.17), channel_id=1, source_target_pairs={{0,16},{16,0},{1,17},{17,1},{2,18},{18,2},{3,19},{19,3},{4,20},{20... | collective-permute-start | bytes 73736 | tf_op jit(solution)/shard_map/ppermute | solution.py:23
  4.5 29.7 %all-to-all-start = ((bf16[8,72,384]{2,1,0:T(8,128)(2,1)}), bf16[8,72,384]{2,1,0:T(8,128)(2,1)S(1)}, u32[]{:S(2)}, u32[]{:S(2)}) async-start(bf16[8,72,384]{2,1,0:T(8,128)(2,1)} %get-tuple-element.26), calls=%async_computation | async-start | bytes 884736 | tf_op jit(solution)/shard_map/all_to_all | solution.py:450
  10.8 12.3 %collective-permute-start.1 = (bf16[1,128,512]{2,1,0:T(8,128)(2,1)S(1)}, bf16[1,128,512]{2,1,0:T(8,128)(2,1)S(1)}, u32[]{:S(2)}, u32[]{:S(2)}) collective-permute-start(bf16[1,128,512]{2,1,0:T(8,128)(2,1)S(1)} %bitcast.4), channel_id=1, source_target_pairs={{0,4},{2,6},{4,0},{6,2},{8,12},{10,14},{12,8},{14,10},{1,5},{3,7},... | collective-permute-start | bytes 393224 | tf_op jit(solution)/shard_map/ppermute | solution.py:23
  11.3 17.6 %collective-permute-start.6 = (bf16[1,128,512]{2,1,0:T(8,128)(2,1)S(1)}, bf16[1,128,512]{2,1,0:T(8,128)(2,1)S(1)}, u32[]{:S(2)}, u32[]{:S(2)}) collective-permute-start(bf16[1,128,512]{2,1,0:T(8,128)(2,1)S(1)} %bitcast.5), channel_id=1, source_target_pairs={{0,8},{2,10},{4,12},{6,14},{8,0},{10,2},{12,4},{14,6},{1,9},{3,11}... | collective-permute-start | bytes 393224 | tf_op jit(solution)/shard_map/ppermute | solution.py:23
  13.7 19.9 %collective-permute-start.7 = (bf16[1,128,512]{2,1,0:T(8,128)(2,1)S(1)}, bf16[1,128,512]{2,1,0:T(8,128)(2,1)S(1)}, u32[]{:S(2)}, u32[]{:S(2)}) collective-permute-start(bf16[1,128,512]{2,1,0:T(8,128)(2,1)S(1)} %bitcast.6), channel_id=1, source_target_pairs={{0,12},{2,14},{4,8},{6,10},{8,4},{10,6},{12,0},{14,2},{1,13},{3,15... | collective-permute-start | bytes 393224 | tf_op jit(solution)/shard_map/ppermute | solution.py:23
  23.1 12.4 %collective-permute-start.2 = (bf16[2,128,512]{2,1,0:T(8,128)(2,1)S(1)}, bf16[2,128,512]{2,1,0:T(8,128)(2,1)S(1)}, u32[]{:S(2)}, u32[]{:S(2)}) collective-permute-start(bf16[2,128,512]{2,1,0:T(8,128)(2,1)S(1)} %pad_maximum_fusion), channel_id=1, source_target_pairs={{0,2},{2,0},{4,6},{6,4},{8,10},{10,8},{12,14},{14,12},{1,3},{3,1},... | collective-permute-start | bytes 786440 | tf_op jit(solution)/shard_map/ppermute | solution.py:23
  33.6 7.4 %collective-permute-start.8 = (bf16[2,128,512]{2,1,0:T(8,128)(2,1)S(1)}, bf16[2,128,512]{2,1,0:T(8,128)(2,1)S(1)}, u32[]{:S(2)}, u32[]{:S(2)}) collective-permute-start(bf16[2,128,512]{2,1,0:T(8,128)(2,1)S(1)} %pad_maximum_fusion.1), channel_id=1, source_target_pairs={{0,2},{2,0},{4,6},{6,4},{8,10},{10,8},{12,14},{14,12},{1,3},{3,1},... | collective-permute-start | bytes 786440 | tf_op jit(solution)/shard_map/ppermute | solution.py:23
  41.6 21.0 %collective-permute-start.9 = (f32[192,512]{1,0:T(8,128)S(1)}, f32[192,512]{1,0:T(8,128)S(1)}, u32[]{:S(2)}, u32[]{:S(2)}) collective-permute-start(f32[192,512]{1,0:T(8,128)S(1)} %shard_map.74), channel_id=1, source_target_pairs={{0,16},{16,0},{1,17},{17,1},{2,18},{18,2},{3,19},{19,3},{4,20},{20... | collective-permute-start | bytes 1179656 | tf_op jit(solution)/shard_map/ppermute | solution.py:33
  41.6 6.5 %collective-permute-start.3 = (bf16[16,512]{1,0:T(8,128)(2,1)S(1)}, bf16[16,512]{1,0:T(8,128)(2,1)S(1)}, u32[]{:S(2)}, u32[]{:S(2)}) collective-permute-start(bf16[16,512]{1,0:T(8,128)(2,1)S(1)} %get-tuple-element.20), channel_id=1, source_target_pairs={{2,4},{4,2},{6,8},{8,6},{10,12},{12,10},{3,5},{5,3},{7,9},{9,7},{1... | collective-permute-start | bytes 49160 | tf_op jit(solution)/shard_map/ppermute | solution.py:453
  52.4 1.3 %collective-permute-start.4 = (f32[3,4,2,384]{3,2,1,0:T(2,128)S(1)}, f32[3,4,2,384]{3,2,1,0:T(2,128)S(1)}, u32[]{:S(2)}, u32[]{:S(2)}) collective-permute-start(f32[3,4,2,384]{3,2,1,0:T(2,128)S(1)} %get-tuple-element.23), channel_id=1, source_target_pairs={{0,16},{16,0},{1,17},{17,1},{2,18},{18,2},{3,19},{19,3},{4,20},{20... | collective-permute-start | bytes 110600 | tf_op jit(solution)/shard_map/ppermute | solution.py:23
  53.7 7.6 %collective-permute-start.5 = (f32[3,2,24,384]{3,2,1,0:T(8,128)S(1)}, f32[3,2,24,384]{3,2,1,0:T(8,128)S(1)}, u32[]{:S(2)}, u32[]{:S(2)}) collective-permute-start(f32[3,2,24,384]{3,2,1,0:T(8,128)S(1)} %bitcast.10), channel_id=1, source_target_pairs={{0,1},{1,0},{2,3},{3,2},{4,5},{5,4},{6,7},{7,6},{8,9},{9,8},{10,11... | collective-permute-start | bytes 663560 | tf_op jit(solution)/shard_map/ppermute | solution.py:33

commit v2 on v1

--- a/solution.py
+++ b/solution.py
@@ -312,7 +312,11 @@
             out[:, :, height - LAP :] += rims[1][:, at]
 
 
-def unfold_kernel(dims, offsets, slab_ref, spread_ref, a_ref):
+def table_kernel(cols, out_ref):
+    out_ref[...] = unfold_matrix(cols)
+
+
+def unfold_kernel(dims, offsets, slab_ref, spread_ref, table_ref, a_ref):
     groups, cols, touched = dims
     nr, nc = lax.axis_size("row"), lax.axis_size("col")
     me = lax.axis_index("col")
@@ -328,7 +332,7 @@
         mixed = jnp.where((lane >= 128 - LAP) & (c > 0), before, 0.0)
         mixed = jnp.where((lane < LAP) & (c < nc - 1), after, mixed)
         wide.append(jnp.concatenate([mine, mixed.astype(mine.dtype)], axis=1))
-    flat = jnp.dot(jnp.concatenate(wide, axis=0), unfold_matrix(cols), preferred_element_type=jnp.float32)
+    flat = jnp.dot(jnp.concatenate(wide, axis=0), table_ref[...], preferred_element_type=jnp.float32)
     u = [
         jnp.dot(
             spread_ref[...],
@@ -464,10 +468,7 @@
     else:
         rims = [shift(rims[1], "row", 1), shift(rims[0], "row", -1)]
     keep, send = call(
-        functools.partial(rim_kernel, (nm, nr)),
-        (keep, send, *rims),
-        [f32(*keep.shape), f32(*send.shape)],
-        6,
+        functools.partial(rim_kernel, (nm, nr)), (keep, send, *rims), [f32(*keep.shape), f32(*send.shape)], 6
     )
     video_grad = keep
     for s in range(1, nm):
@@ -475,9 +476,10 @@
         video_grad = video_grad + part
 
     share = touched * KS
+    (matrix,) = call(functools.partial(table_kernel, cols), (), [bf16(width + 128, KS * cols)], 4)
     (unfolded,) = call(
         functools.partial(unfold_kernel, (groups, cols, touched), tuple(offsets)),
-        (slabs, spread),
+        (slabs, spread, matrix),
         [bf16(nr, share, groups * nc * cols)],
         10,
         flops=2 * nc * groups * units * (width + 128) * KS * cols,

time: 63.6 us -> 64.5 us (1.014)
  other arithmetic: 1.58 us -> 2.28 us
    concatenate x2, other arithmetic: 0.05 us -> 0.75 us  [joined(): return parts[0] if len(parts) == 1 else jnp.concatenate(parts, axis=0)]
    pallas_call x7 -> x8, Pallas kernels: 9.14 us -> 9.24 us  [call(): pl.pallas_call(kernel, in_specs=[pl.BlockSpec(memory_space=space(k, hbm))...]
  transfers between devices with their start and end apart: 11 -> 11, of which waited for: 8 -> 8; matrix products, arithmetic and copies ran while one was open for 1% -> 2% of each run, Pallas kernels for 9% -> 10%
where the time goes in v2:
time: 64.5 us; the launch traced here: 64.2 us
  waiting for transfers between devices  37.7 us (58%)
  starting transfers between devices  14.2 us (22%)
  Pallas kernels  9.24 us (14%)
  other arithmetic  2.28 us (4%)
  between operations  0.76 us (1%)
    ppermute x7, waiting for transfers between devices, swap(): return lax.ppermute(x, axis, [(i, i ^ bit) for i in range(n)])  27.2 us
    pallas_call x8, Pallas kernels, call(): pl.pallas_call(kernel, in_specs=[pl.BlockSpec(memory_space=space(k, hbm))...  9.24 us
    ppermute x2, waiting for transfers between devices, rotate(): return lax.ppermute(x, axis, [(i, (i + by) % n) for i in range(n)])  7 us
    all_to_all x1, starting transfers between devices, both_gradients(): slabs = lax.all_to_all(slabs, 'col', 0, 0, tiled=True)  6.23 us
    ppermute x7, starting transfers between devices, swap(): return lax.ppermute(x, axis, [(i, i ^ bit) for i in range(n)])  4.26 us
    ppermute x1, waiting for transfers between devices, both_gradients(): edge = lax.ppermute(edge, 'col', ring)  3.43 us
    ppermute x1, starting transfers between devices, both_gradients(): edge = lax.ppermute(edge, 'col', ring)  3.09 us
  transfers between devices with their start and end apart: 11, of which 8 were waited for; matrix products, arithmetic and copies ran while one was open for 2% of the time, Pallas kernels for 10%

profile of v2, /device:TPU:14, one launch (start us, length us, event | category | flops | bytes accessed | tf_op | source)
XLA Modules:
  0.0 64.2 jit_solution(12820711160097936371)
XLA Ops:
  0.6 1.2 %shard_map.68 = (bf16[288,384]{1,0:T(8,128)(2,1)S(1)}, bf16[128,512]{1,0:T(8,128)(2,1)S(1)}, bf16[8,72,352]{2,1,0:T(8,128)(2,1)S(1)}, bf16[96,72]{1,0:T(8,128)(2...) custom-call(bf16[288,384]{1,0:T(8,128)(2,1)} %bitcast.11, bf16[128,512]{1,0:T(8,128)(2,1)} %bitcast.12, ...), custom_call_target="tpu_custom_call" | custom-call | flops 1048576 | bytes 1048576 | tf_op jit(solution)/shard_map/pallas_call | solution.py:394
  2.0 1.2 %collective-permute-done.refs_0_ = bf16[32,384]{1,0:T(8,128)(2,1)S(1)} collective-permute-done((bf16[32,384]{1,0:T(8,128)(2,1)S(1)}, bf16[32,384]{1,0:T(8,128)(2,1)S(1)}, u32[]{:S(2)}, u32[]{:S(2)}) %collective-permute-start) | collective-permute-done | bytes 24608 | tf_op jit(solution)/shard_map/ppermute | solution.py:23
  3.1 1.4 %shard_map.69 = (bf16[8,72,384]{2,1,0:T(8,128)(2,1)}, bf16[1024,512]{1,0:T(8,128)(2,1)S(1)}) custom-call(bf16[8,72,352]{2,1,0:T(8,128)(2,1)S(1)} %get-tuple-element.15.table_ref, bf16[288,384]{1,0:T(8,128)(2,1)S(1)} %get-tuple-element.16.video_ref, bf16[3072,512]{1,0:T(8,128)(2,1)} %w_ref.1, bf16[32,384]{1,0:T(8,128)(2,1)S(1)} %collective-permute-done.refs_0_), custom_call_target="tpu_custom_call" | custom-call | flops 155713536 | bytes 1048576 | tf_op jit(solution)/shard_map/pallas_call | solution.py:394
  4.5 6.2 %all-to-all-start = ((bf16[8,72,384]{2,1,0:T(8,128)(2,1)}), bf16[8,72,384]{2,1,0:T(8,128)(2,1)S(1)}, u32[]{:S(2)}, u32[]{:S(2)}) async-start(bf16[8,72,384]{2,1,0:T(8,128)(2,1)} %get-tuple-element.26), calls=%async_computation | async-start | bytes 884736 | tf_op jit(solution)/shard_map/all_to_all | solution.py:454
  10.8 0.6 collective-permute-start.1
  11.3 2.4 %collective-permute-start.6 = (bf16[1,128,512]{2,1,0:T(8,128)(2,1)S(1)}, bf16[1,128,512]{2,1,0:T(8,128)(2,1)S(1)}, u32[]{:S(2)}, u32[]{:S(2)}) collective-permute-start(bf16[1,128,512]{2,1,0:T(8,128)(2,1)S(1)} %bitcast.5), channel_id=1, source_target_pairs={{0,8},{2,10},{4,12},{6,14},{8,0},{10,2},{12,4},{14,6},{1,9},{3,11}... | collective-permute-start | bytes 393224 | tf_op jit(solution)/shard_map/ppermute | solution.py:23
  13.7 0.6 collective-permute-start.7
  14.2 8.8 %collective-permute-done.1.refs_1_ = bf16[1,128,512]{2,1,0:T(8,128)(2,1)S(1)} collective-permute-done((bf16[1,128,512]{2,1,0:T(8,128)(2,1)S(1)}, bf16[1,128,512]{2,1,0:T(8,128)(2,1)S(1)}, u32[]{:S(2)}, u32[]{:S(2)}) %collective-permute-start.1) | collective-permute-done | bytes 131104 | tf_op jit(solution)/shard_map/ppermute | solution.py:23
  23.1 5.8 %collective-permute-done.6.refs_2_ = bf16[1,128,512]{2,1,0:T(8,128)(2,1)S(1)} collective-permute-done((bf16[1,128,512]{2,1,0:T(8,128)(2,1)S(1)}, bf16[1,128,512]{2,1,0:T(8,128)(2,1)S(1)}, u32[]{:S(2)}, u32[]{:S(2)}) %collective-permute-start.6) | collective-permute-done | bytes 131104 | tf_op jit(solution)/shard_map/ppermute | solution.py:23
  29.0 4.6 %collective-permute-done.7.refs_3_ = bf16[1,128,512]{2,1,0:T(8,128)(2,1)S(1)} collective-permute-done((bf16[1,128,512]{2,1,0:T(8,128)(2,1)S(1)}, bf16[1,128,512]{2,1,0:T(8,128)(2,1)S(1)}, u32[]{:S(2)}, u32[]{:S(2)}) %collective-permute-start.7) | collective-permute-done | bytes 131104 | tf_op jit(solution)/shard_map/ppermute | solution.py:23
  33.6 0.7 %pad_maximum_fusion.1 = bf16[2,128,512]{2,1,0:T(8,128)(2,1)} fusion(bf16[1,128,512]{2,1,0:T(8,128)(2,1)S(1)} %collective-permute-done.7.refs_3_, bf16[1,128,512]{2,1,0:T(8,128)(2,1)S(1)} %collective-permute-done.6.refs_2_), kind=kLoop, calls=%fused_computation.2 | loop fusion | flops 131072 | bytes 524288 | tf_op jit(solution)/shard_map/concatenate | solution.py:385
  34.3 0.6 collective-permute-start.8
  35.0 1.2 %shard_map.73.a_ref = bf16[2,192,1024]{2,1,0:T(8,128)(2,1)S(1)} custom-call(bf16[8,72,384]{2,1,0:T(8,128)(2,1)S(1)} %all-to-all-done.slab_ref, bf16[96,72]{1,0:T(8,128)(2,1)S(1)} %get-tuple-element.27.spread_ref, bf16[512,512]{1,0:T(8,128)(2,1)S(1)} %shard_map.72.table_ref), custom_call_target="tpu_custom_call" | custom-call | flops 402653184 | bytes 1048576 | tf_op jit(solution)/shard_map/pallas_call | solution.py:394
  36.2 5.6 %collective-permute-done.8.refs_5_ = bf16[2,128,512]{2,1,0:T(8,128)(2,1)S(1)} collective-permute-done((bf16[2,128,512]{2,1,0:T(8,128)(2,1)}, bf16[2,128,512]{2,1,0:T(8,128)(2,1)S(1)}, u32[]{:S(2)}, u32[]{:S(2)}) %collective-permute-start.8) | collective-permute-done | bytes 262176 | tf_op jit(solution)/shard_map/ppermute | solution.py:23
  41.9 0.5 shard_map.75
  42.5 3.1 %collective-permute-start.3 = (bf16[16,512]{1,0:T(8,128)(2,1)S(1)}, bf16[16,512]{1,0:T(8,128)(2,1)S(1)}, u32[]{:S(2)}, u32[]{:S(2)}) collective-permute-start(bf16[16,512]{1,0:T(8,128)(2,1)S(1)} %get-tuple-element.20), channel_id=1, source_target_pairs={{2,4},{4,2},{6,8},{8,6},{10,12},{12,10},{3,5},{5,3},{7,9},{9,7},{1... | collective-permute-start | bytes 49160 | tf_op jit(solution)/shard_map/ppermute | solution.py:457
  45.6 3.4 %collective-permute-done.3.edge_ref = bf16[16,512]{1,0:T(8,128)(2,1)S(1)} collective-permute-done((bf16[16,512]{1,0:T(8,128)(2,1)S(1)}, bf16[16,512]{1,0:T(8,128)(2,1)S(1)}, u32[]{:S(2)}, u32[]{:S(2)}) %collective-permute-start.3) | collective-permute-done | bytes 16416 | tf_op jit(solution)/shard_map/ppermute | solution.py:457
  49.0 4.2 %shard_map.70 = (f32[3,2,24,384]{3,2,1,0:T(8,128)S(1)}, f32[1,3,2,24,384]{4,3,2,1,0:T(8,128)S(1)}, f32[3,4,2,384]{3,2,1,0:T(2,128)S(1)}) custom-call(bf16[1024,512]{1,0:T(8,128)(2,1)S(1)} %get-tuple-element.18.first_ref, bf16[3072,512]{1,0:T(8,128)(2,1)} %w_ref.1, bf16[128,512]{1,0:T(8,128)(2,1)S(1)} %get-tuple-element.19.g_ref, ...), custom_call_target="tpu_custom_call" | custom-call | flops 805306368 | bytes 1048576 | tf_op jit(solution)/shard_map/pallas_call | solution.py:394
  53.3 1.2 %collective-permute-done.4.refs_0_ = f32[3,4,2,384]{3,2,1,0:T(2,128)S(1)} collective-permute-done((f32[3,4,2,384]{3,2,1,0:T(2,128)S(1)}, f32[3,4,2,384]{3,2,1,0:T(2,128)S(1)}, u32[]{:S(2)}, u32[]{:S(2)}) %collective-permute-start.4) | collective-permute-done | bytes 36896 | tf_op jit(solution)/shard_map/ppermute | solution.py:23
  54.5 0.6 collective-permute-start.5
  55.1 7.0 %collective-permute-done.5 = f32[3,2,24,384]{3,2,1,0:T(8,128)S(1)} collective-permute-done((f32[3,2,24,384]{3,2,1,0:T(8,128)S(1)}, f32[3,2,24,384]{3,2,1,0:T(8,128)S(1)}, u32[]{:S(2)}, u32[]{:S(2)}) %collective-permute-start.5) | collective-permute-done | bytes 221216 | tf_op jit(solution)/shard_map/ppermute | solution.py:33
  62.1 0.7 %add.6 = f32[3,2,24,384]{3,2,1,0:T(8,128)} add(f32[3,2,24,384]{3,2,1,0:T(8,128)S(1)} %get-tuple-element.24, f32[3,2,24,384]{3,2,1,0:T(8,128)S(1)} %collective-permute-done.5) | non-fusion elementwise | flops 55296 | bytes 663552 | tf_op jit(solution)/shard_map/add | solution.py:476
  62.8 0.5 shard_map.74
  63.4 0.8 %add_multiply_fusion = f32[192,512]{1,0:T(8,128)} fusion(f32[192,512]{1,0:T(8,128)S(1)} %shard_map.74, f32[192,512]{1,0:T(8,128)S(1)} %collective-permute-done.9), kind=kLoop, calls=%fused_computation | loop fusion | flops 196608 | bytes 1179648 | tf_op jit(solution)/shard_map/mul | solution.py:501
  (10 shorter events, 0.5 us)
Async XLA Ops:
  1.9 1.3 %collective-permute-start = (bf16[32,384]{1,0:T(8,128)(2,1)S(1)}, bf16[32,384]{1,0:T(8,128)(2,1)S(1)}, u32[]{:S(2)}, u32[]{:S(2)}) collective-permute-start(bf16[32,384]{1,0:T(8,128)(2,1)S(1)} %get-tuple-element.17), channel_id=1, source_target_pairs={{0,16},{16,0},{1,17},{17,1},{2,18},{18,2},{3,19},{19,3},{4,20},{20... | collective-permute-start | bytes 73736 | tf_op jit(solution)/shard_map/ppermute | solution.py:23
  4.5 30.5 %all-to-all-start = ((bf16[8,72,384]{2,1,0:T(8,128)(2,1)}), bf16[8,72,384]{2,1,0:T(8,128)(2,1)S(1)}, u32[]{:S(2)}, u32[]{:S(2)}) async-start(bf16[8,72,384]{2,1,0:T(8,128)(2,1)} %get-tuple-element.26), calls=%async_computation | async-start | bytes 884736 | tf_op jit(solution)/shard_map/all_to_all | solution.py:454
  10.8 12.3 %collective-permute-start.1 = (bf16[1,128,512]{2,1,0:T(8,128)(2,1)S(1)}, bf16[1,128,512]{2,1,0:T(8,128)(2,1)S(1)}, u32[]{:S(2)}, u32[]{:S(2)}) collective-permute-start(bf16[1,128,512]{2,1,0:T(8,128)(2,1)S(1)} %bitcast.4), channel_id=1, source_target_pairs={{0,4},{2,6},{4,0},{6,2},{8,12},{10,14},{12,8},{14,10},{1,5},{3,7},... | collective-permute-start | bytes 393224 | tf_op jit(solution)/shard_map/ppermute | solution.py:23
  11.3 17.6 %collective-permute-start.6 = (bf16[1,128,512]{2,1,0:T(8,128)(2,1)S(1)}, bf16[1,128,512]{2,1,0:T(8,128)(2,1)S(1)}, u32[]{:S(2)}, u32[]{:S(2)}) collective-permute-start(bf16[1,128,512]{2,1,0:T(8,128)(2,1)S(1)} %bitcast.5), channel_id=1, source_target_pairs={{0,8},{2,10},{4,12},{6,14},{8,0},{10,2},{12,4},{14,6},{1,9},{3,11}... | collective-permute-start | bytes 393224 | tf_op jit(solution)/shard_map/ppermute | solution.py:23
  13.7 19.9 %collective-permute-start.7 = (bf16[1,128,512]{2,1,0:T(8,128)(2,1)S(1)}, bf16[1,128,512]{2,1,0:T(8,128)(2,1)S(1)}, u32[]{:S(2)}, u32[]{:S(2)}) collective-permute-start(bf16[1,128,512]{2,1,0:T(8,128)(2,1)S(1)} %bitcast.6), channel_id=1, source_target_pairs={{0,12},{2,14},{4,8},{6,10},{8,4},{10,6},{12,0},{14,2},{1,13},{3,15... | collective-permute-start | bytes 393224 | tf_op jit(solution)/shard_map/ppermute | solution.py:23
  23.1 13.2 %collective-permute-start.2 = (bf16[2,128,512]{2,1,0:T(8,128)(2,1)S(1)}, bf16[2,128,512]{2,1,0:T(8,128)(2,1)S(1)}, u32[]{:S(2)}, u32[]{:S(2)}) collective-permute-start(bf16[2,128,512]{2,1,0:T(8,128)(2,1)S(1)} %pad_maximum_fusion), channel_id=1, source_target_pairs={{0,2},{2,0},{4,6},{6,4},{8,10},{10,8},{12,14},{14,12},{1,3},{3,1},... | collective-permute-start | bytes 786440 | tf_op jit(solution)/shard_map/ppermute | solution.py:23
  34.3 7.5 %collective-permute-start.8 = (bf16[2,128,512]{2,1,0:T(8,128)(2,1)}, bf16[2,128,512]{2,1,0:T(8,128)(2,1)S(1)}, u32[]{:S(2)}, u32[]{:S(2)}) collective-permute-start(bf16[2,128,512]{2,1,0:T(8,128)(2,1)} %pad_maximum_fusion.1), channel_id=1, source_target_pairs={{0,2},{2,0},{4,6},{6,4},{8,10},{10,8},{12,14},{14,12},{1,3},{3,1},... | collective-permute-start | bytes 786440 | tf_op jit(solution)/shard_map/ppermute | solution.py:23
  42.4 21.0 %collective-permute-start.9 = (f32[192,512]{1,0:T(8,128)S(1)}, f32[192,512]{1,0:T(8,128)S(1)}, u32[]{:S(2)}, u32[]{:S(2)}) collective-permute-start(f32[192,512]{1,0:T(8,128)S(1)} %shard_map.75), channel_id=1, source_target_pairs={{0,16},{16,0},{1,17},{17,1},{2,18},{18,2},{3,19},{19,3},{4,20},{20... | collective-permute-start | bytes 1179656 | tf_op jit(solution)/shard_map/ppermute | solution.py:33
  42.5 6.5 %collective-permute-start.3 = (bf16[16,512]{1,0:T(8,128)(2,1)S(1)}, bf16[16,512]{1,0:T(8,128)(2,1)S(1)}, u32[]{:S(2)}, u32[]{:S(2)}) collective-permute-start(bf16[16,512]{1,0:T(8,128)(2,1)S(1)} %get-tuple-element.20), channel_id=1, source_target_pairs={{2,4},{4,2},{6,8},{8,6},{10,12},{12,10},{3,5},{5,3},{7,9},{9,7},{1... | collective-permute-start | bytes 49160 | tf_op jit(solution)/shard_map/ppermute | solution.py:457
  53.2 1.3 %collective-permute-start.4 = (f32[3,4,2,384]{3,2,1,0:T(2,128)S(1)}, f32[3,4,2,384]{3,2,1,0:T(2,128)S(1)}, u32[]{:S(2)}, u32[]{:S(2)}) collective-permute-start(f32[3,4,2,384]{3,2,1,0:T(2,128)S(1)} %get-tuple-element.23), channel_id=1, source_target_pairs={{0,16},{16,0},{1,17},{17,1},{2,18},{18,2},{3,19},{19,3},{4,20},{20... | collective-permute-start | bytes 110600 | tf_op jit(solution)/shard_map/ppermute | solution.py:23
  54.5 7.6 %collective-permute-start.5 = (f32[3,2,24,384]{3,2,1,0:T(8,128)S(1)}, f32[3,2,24,384]{3,2,1,0:T(8,128)S(1)}, u32[]{:S(2)}, u32[]{:S(2)}) collective-permute-start(f32[3,2,24,384]{3,2,1,0:T(8,128)S(1)} %bitcast.10), channel_id=1, source_target_pairs={{0,1},{1,0},{2,3},{3,2},{4,5},{5,4},{6,7},{7,6},{8,9},{9,8},{10,11... | collective-permute-start | bytes 663560 | tf_op jit(solution)/shard_map/ppermute | solution.py:33
